TPU v7x, 32 devices: a whole 2x2x4 slice. The times are simulated.
32 devices in a mesh: pts: 8 (over z, core), head: 4 (over y, x).
Axes of the slice: x: 2, y: 2, z: 4, core: 2. Of those that a mesh axis runs over, the one named last changes fastest.
Arguments:
- points: bfloat16 [73728, 128], P('pts')
- counts: int32 [8], P('pts'), may hold values from 1 to 9216, 55296 in all
- ln1_gain: float32 [2, 128], replicated, may hold values from 0.5 to 1.5
- ln1_bias: float32 [2, 128], replicated, may hold values from -1.5 to 1.5
- w_in: bfloat16 [2, 128, 128], P(None, None, 'head'), may hold values from -0.5 to 0.5
- w_fx: bfloat16 [2, 128, 128], P(None, None, 'head'), may hold values from -0.5 to 0.5
- w_slice: bfloat16 [2, 32, 32], replicated
- temper: float32 [2, 4], replicated, may hold values from 0.5 to 2
- query_weight: bfloat16 [2, 32, 32], replicated
- key_weight: bfloat16 [2, 32, 32], replicated, may hold values from -1 to 1
- value_weight: bfloat16 [2, 32, 32], replicated, may hold values from -1 to 1
- w_out: bfloat16 [2, 128, 128], P(None, 'head'), may hold values from -1 to 1
- b_out: float32 [2, 128], replicated, may hold values from -1.5 to 1.5
- ln2_gain: float32 [2, 128], replicated, may hold values from 0.5 to 1.5
- ln2_bias: float32 [2, 128], replicated, may hold values from -1.5 to 1.5
- w_up: bfloat16 [2, 128, 512], replicated, may hold values from -0.5 to 0.5
- w_down: bfloat16 [2, 512, 128], replicated, may hold values from -0.25 to 0.25
Outputs:
- features: bfloat16 [73728, 128], P(('pts', 'head'))
Inputs may be any that keep to these rules, and one draw needn't show every extreme that they name: counts[i] live points fill the first slots of shard i; at least one shard is full; they sum to 55296.
All inputs are finite; a program needn't handle non-finite values.
Results may differ from a plain program's by a relative error of at most 0.014.
Values may be sent and summed in bfloat16 or wider, within the bound.
A program may use at most 128 MiB of HBM per device.

v0:
```python
import jax
import jax.numpy as jnp
from jax import lax
from jax.sharding import PartitionSpec as P

DH = 32
M = 32


def layer_norm(value, gain, bias):
    mean = jnp.mean(value, axis=-1, keepdims=True)
    centred = value - mean
    var = jnp.mean(centred * centred, axis=-1, keepdims=True)
    return centred * lax.rsqrt(var + 1e-05) * gain + bias


def slice_attention(token_rows, query_weight, key_weight, value_weight):
    head_parts = lax.Precision.HIGHEST
    query_rows = jnp.einsum(
        "aur,rz->auz", token_rows, query_weight.astype(jnp.float32), precision=head_parts
    )
    slice_keys = jnp.einsum(
        "aur,rz->auz", token_rows, key_weight.astype(jnp.float32), precision=head_parts
    )
    slice_values = jnp.einsum(
        "aur,rz->auz", token_rows, value_weight.astype(jnp.float32), precision=head_parts
    )
    scores = jnp.einsum("hme,hke->hmk", query_rows, slice_keys, precision=head_parts) * DH ** (-0.5)
    attn = jax.nn.softmax(scores, axis=-1)
    return jnp.einsum("hmk,hke->hme", attn, slice_values, precision=head_parts).astype(jnp.bfloat16)


def body(
    points,
    counts,
    ln1_gain,
    ln1_bias,
    w_in,
    w_fx,
    w_slice,
    temper,
    query_weight,
    key_weight,
    value_weight,
    w_out,
    b_out,
    ln2_gain,
    ln2_bias,
    w_up,
    w_down,
):
    groups = lax.axis_size("head")
    rows = points.shape[0] // groups
    first_row = lax.axis_index("head") * rows
    layers = w_in.shape[0]
    full_in = lax.all_gather(w_in, "head", axis=2, tiled=True)
    full_fx = lax.all_gather(w_fx, "head", axis=2, tiled=True)
    full_out = lax.all_gather(w_out, "head", axis=1, tiled=True)
    heads = full_in.shape[2] // DH
    live = (first_row + jnp.arange(rows, dtype=jnp.int32) < counts[0]).astype(jnp.float32)
    current = lax.dynamic_slice_in_dim(points, first_row, rows, 0)
    for layer_index in range(layers):
        normed = layer_norm(
            current.astype(jnp.float32), ln1_gain[layer_index], ln1_bias[layer_index]
        ).astype(jnp.bfloat16)
        mid = jnp.dot(normed, full_in[layer_index], preferred_element_type=jnp.float32).astype(
            jnp.bfloat16
        )
        feats = jnp.dot(normed, full_fx[layer_index], preferred_element_type=jnp.float32).astype(
            jnp.bfloat16
        )
        spread = jnp.kron(jnp.eye(heads, dtype=jnp.bfloat16), w_slice[layer_index])
        logits = jnp.dot(mid, spread, preferred_element_type=jnp.float32)
        logits = logits.reshape(rows, heads, M) / temper[layer_index][None, :, None]
        weights = jax.nn.softmax(logits, axis=-1) * live[:, None, None]
        half_weights = weights.astype(jnp.bfloat16).reshape(rows, heads * M)
        total = jnp.sum(weights, axis=0)
        square = jnp.einsum("rs,rl->sl", half_weights, feats, preferred_element_type=jnp.float32)
        square = square.reshape(heads, M, heads, DH)
        numerator = jnp.stack([square[h, :, h, :] for h in range(heads)])
        numerator, total = lax.psum((numerator, total), ("pts", "head"))
        token_rows = numerator / jnp.maximum(total, 1.0)[..., None]
        mixed_token = slice_attention(
            token_rows,
            query_weight[layer_index],
            key_weight[layer_index],
            value_weight[layer_index],
        )
        wide = (
            jnp.einsum(
                "hmv,hvc->hmc",
                mixed_token,
                full_out[layer_index].reshape(heads, DH, -1),
                preferred_element_type=jnp.float32,
            )
            .astype(jnp.bfloat16)
            .reshape(heads * M, -1)
        )
        projected = jnp.dot(half_weights, wide, preferred_element_type=jnp.float32)
        after = current.astype(jnp.float32) + projected + b_out[layer_index]
        normed2 = layer_norm(after, ln2_gain[layer_index], ln2_bias[layer_index]).astype(
            jnp.bfloat16
        )
        upper = jax.nn.gelu(
            jnp.dot(normed2, w_up[layer_index], preferred_element_type=jnp.float32)
        ).astype(jnp.bfloat16)
        current = (
            after + jnp.dot(upper, w_down[layer_index], preferred_element_type=jnp.float32)
        ).astype(jnp.bfloat16)
    return current


def solution(mesh):
    placed = (
        P("pts", None),
        P("pts"),
        P(),
        P(),
        P(None, None, "head"),
        P(None, None, "head"),
        P(),
        P(),
        P(),
        P(),
        P(),
        P(None, "head", None),
        P(),
        P(),
        P(),
        P(),
        P(),
    )
    return jax.shard_map(
        body, mesh=mesh, in_specs=placed, out_specs=P(("pts", "head"), None), check_vma=False
    )
```

profile of v0, /device:TPU:0, one launch (start us, length us, event | category | flops | bytes accessed | tf_op | source)
XLA Modules:
  0.0 157.5 jit_solution(5383199505180625222)
XLA Ops:
  0.0 1.7 %copy-done = bf16[9216,128]{1,0:T(8,128)(2,1)S(1)} copy-done((bf16[9216,128]{1,0:T(8,128)(2,1)S(1)}, bf16[9216,128]{1,0:T(8,128)(2,1)}, u32[]{:S(2)}) %copy-start) | copy-done | bytes 2359320
  1.7 0.0 copy-start.13
  1.7 0.2 copy.26
  2.0 0.0 copy-start.18
  2.0 0.0 copy-start.19
  2.0 0.0 copy-start.10
  2.0 0.0 copy-start.16
  2.0 0.1 convert_reduce_fusion
  2.1 0.2 fusion.33
  2.3 0.3 copy-done.18
  2.7 0.0 copy-done.19
  2.7 0.6 slice_bitcast_fusion.34
  3.3 0.1 copy.19
  3.4 0.1 copy.20
  3.5 0.8 broadcast_multiply_fusion
  4.3 0.1 mul.187
  4.4 9.7 %all_gather.9 = bf16[2,128,128]{1,2,0:T(8,128)(2,1)S(1)} all-gather(bf16[2,128,32]{1,2,0:T(8,128)(2,1)S(1)} %copy-done.10), channel_id=1, replica_groups=mesh['pts'=8,'head'=4] {'head'}, dimensions={2}, use_global_device_ids=true | all-gather | bytes 81920 | tf_op jit(solution)/shard_map/all_gather | solution.py:56
  14.2 1.9 %fusion.122 = (f32[2304,4]{0,1:T(4,128)S(1)}, f32[2304,4,32]{0,2,1:T(8,128)}) fusion(bf16[4,32,128]{2,1,0:T(8,128)(2,1)S(1)} %bitcast.209, f32[4]{0:T(128)S(1)} %get-tuple-element.28, bf16[2,128,128]{1,2,0:T(8,128)(2,1)S(1)} %all_gather.9, bf16[2304,128]{0,1:T(8,128)(2,1)S(1)} %copy.26, f32[128]{0:T(128)S(1)} %get-tuple-element.34, ...), kind=kOutput, calls=%fused_computation.175 | convolution fusion | flops 153944096 | bytes 1897984 | tf_op jit(solution)/shard_map/sub | solution.py:75
  16.0 0.0 copy-start.11
  16.7 1.6 %fusion.57 = f32[4,32]{1,0:T(4,128)S(1)} fusion(f32[2304]{0:T(1024)S(1)} %fusion.83, f32[2304,4,32]{0,2,1:T(8,128)} %get-tuple-element.36, f32[2304,4]{0,1:T(4,128)S(1)} %get-tuple-element.35), kind=kLoop, calls=%fused_computation.77 | loop fusion | flops 884608 | bytes 1226240 | tf_op jit(solution)/shard_map/reduce_sum | solution.py:77
  18.3 8.2 %all_gather.10 = bf16[2,128,128]{1,2,0:T(8,128)(2,1)S(1)} all-gather(bf16[2,128,32]{1,2,0:T(8,128)(2,1)S(1)} %copy-done.11), channel_id=1, replica_groups=mesh['pts'=8,'head'=4] {'head'}, dimensions={2}, use_global_device_ids=true | all-gather | bytes 81920 | tf_op jit(solution)/shard_map/all_gather | solution.py:57
  26.5 0.4 convolution_convert_fusion.1
  27.0 0.0 copy-start.23
  27.0 0.0 copy-start.24
  27.0 0.0 copy-start.25
  27.0 0.6 fusion.39
  27.6 0.0 copy-start.12
  27.6 0.0 copy-start.17
  27.7 40.2 %all-reduce.1 = (f32[4,32,32]{2,1,0:T(8,128)S(1)}, f32[4,32]{1,0:T(4,128)S(1)}) all-reduce(f32[4,32,32]{2,1,0:T(8,128)S(1)} %pad_maximum_fusion, f32[4,32]{1,0:T(4,128)S(1)} %fusion.57), channel_id=1, replica_groups=mesh['pts'=8,'head'=4] {'pts','head'}, use_global_device_ids=true, to_apply=%region_4.5 | all-reduce | flops 4224 | bytes 33792 | tf_op jit(solution)/shard_map/psum | solution.py:81
  67.9 0.2 fusion.92
  68.2 0.2 fusion.94
  68.4 0.2 fusion.125
  68.7 0.2 fusion.90
  69.0 0.3 convolution_convert_fusion.7
  69.3 9.0 %all_gather.11 = bf16[2,128,128]{2,1,0:T(8,128)(2,1)S(1)} all-gather(bf16[2,32,128]{2,1,0:T(8,128)(2,1)S(1)} %copy-done.12), channel_id=1, replica_groups=mesh['pts'=8,'head'=4] {'head'}, dimensions={1}, use_global_device_ids=true | all-gather | bytes 81920 | tf_op jit(solution)/shard_map/all_gather | solution.py:58
  78.3 0.6 fusion.121
  78.9 0.5 slice_bitcast_fusion.32
  79.4 2.8 %fusion.126 = (f32[2304]{0:T(1024)S(1)}, f32[2304,128]{0,1:T(8,128)}) fusion(f32[128]{0:T(128)S(1)} %get-tuple-element.26, bf16[4,32,32]{2,1,0:T(8,128)(2,1)S(1)} %convolution_convert_fusion.7, bf16[4,32,128]{2,1,0:T(8,128)(2,1)S(1)} %bitcast.212, f32[2304]{0:T(1024)S(1)} %fusion.83, f32[2304,4,32]{0,2,1:T(8,128)} %get-tuple-element.36, ...), kind=kOutput, calls=%fused_computation.177 | convolution fusion | flops 78624512 | bytes 3045888 | tf_op jit(solution)/shard_map/dot_general | solution.py:99
  82.2 1.4 multiply_reduce_fusion.2
  83.6 0.6 add_rsqrt_fusion.2
  84.2 0.6 slice_bitcast_fusion.30
  84.8 4.6 %fusion.127 = (f32[2304]{0:T(1024)}, f32[2304,128]{0,1:T(8,128)S(1)}) fusion(f32[2304,128]{0,1:T(8,128)} %get-tuple-element.40, bf16[2,512,128]{2,1,0:T(8,128)(2,1)} %param.33, f32[128]{0:T(128)} %get-tuple-element.24, f32[128]{0:T(128)} %get-tuple-element.51, f32[2304]{0:T(1024)} %add_rsqrt_fusion.2, f32[2304]{0:T(1024)} %copy-done.8, ...), kind=kOutput, calls=%fused_computation.178 | convolution fusion | flops 617248512 | bytes 3835904 | tf_op jit(solution)/shard_map/dot_general | solution.py:108
  89.4 0.7 broadcast_multiply_fusion.3
  90.1 0.1 multiply_reduce_fusion.1
  90.3 1.2 add_convert_fusion.1
  91.5 1.6 %mul.210 = bf16[128,128]{0,1:T(8,128)(2,1)} reshape(bf16[4,32,4,32]{1,0,3,2:T(4,128)(2,1)} %get-tuple-element.29) | data formatting | bytes 65536 | tf_op jit(solution)/shard_map/jit(kron)/mul | solution.py:72
  93.1 3.4 %fusion.130 = (f32[2304,4]{0,1:T(4,128)}, f32[2304,4,32]{0,2,1:T(8,128)}) fusion(bf16[4,32,128]{2,1,0:T(8,128)(2,1)} %bitcast.210, bf16[2304,128]{0,1:T(8,128)(2,1)} %add_convert_fusion.1, f32[4]{0:T(128)S(1)} %get-tuple-element.27, bf16[2,128,128]{1,2,0:T(8,128)(2,1)} %copy-done.7), kind=kOutput, calls=%fused_computation.179 | convolution fusion | flops 152174624 | bytes 1871888 | tf_op jit(solution)/shard_map/sub | solution.py:75
  96.5 1.6 %fusion.59 = f32[4,32]{1,0:T(4,128)S(1)} fusion(f32[2304]{0:T(1024)S(1)} %fusion.83, f32[2304,4,32]{0,2,1:T(8,128)} %get-tuple-element.44, f32[2304,4]{0,1:T(4,128)} %get-tuple-element.43), kind=kLoop, calls=%fused_computation.79 | loop fusion | flops 884608 | bytes 1226240 | tf_op jit(solution)/shard_map/reduce_sum | solution.py:77
  98.2 0.3 convolution_convert_fusion
  98.5 0.6 fusion.37
  99.1 0.6 pad_maximum_fusion.1
  99.7 40.3 %all-reduce = (f32[4,32,32]{2,1,0:T(8,128)}, f32[4,32]{1,0:T(4,128)}) all-reduce(f32[4,32,32]{2,1,0:T(8,128)} %pad_maximum_fusion.1, f32[4,32]{1,0:T(4,128)S(1)} %fusion.59), channel_id=1, replica_groups=mesh['pts'=8,'head'=4] {'pts','head'}, use_global_device_ids=true, to_apply=%region_15.16 | all-reduce | flops 4224 | bytes 33792 | tf_op jit(solution)/shard_map/psum | solution.py:81
  140.0 0.7 broadcast_maximum_fusion
  140.7 1.1 fusion.86
  141.8 1.1 fusion.88
  142.9 0.2 fusion.131
  143.1 1.1 fusion.84
  144.2 0.9 convolution_convert_fusion.5
  145.2 3.4 %fusion.132 = (f32[2304]{0:T(1024)}, f32[2304,128]{0,1:T(8,128)}) fusion(f32[128]{0:T(128)} %get-tuple-element.25, f32[2304,128]{0,1:T(8,128)S(1)} %get-tuple-element.42, bf16[4,32,32]{2,1,0:T(8,128)(2,1)} %convolution_convert_fusion.5, bf16[4,32,128]{2,1,0:T(8,128)(2,1)} %bitcast.211, f32[2304]{0:T(1024)S(1)} %fusion.83, ...), kind=kOutput, calls=%fused_computation.181 | convolution fusion | flops 78329600 | bytes 3635712 | tf_op jit(solution)/shard_map/dot_general | solution.py:99
  148.6 0.8 broadcast_multiply_fusion.2
  149.4 1.4 multiply_reduce_fusion
  150.8 0.6 add_rsqrt_fusion
  151.4 4.0 %fusion.27 = bf16[2304,128]{0,1:T(8,128)(2,1)} fusion(f32[2304,128]{0,1:T(8,128)S(1)} %copy-done.4, f32[128]{0:T(128)S(1)} %copy-done.22, f32[128]{0:T(128)} %get-tuple-element.52, f32[2304]{0:T(1024)} %add_rsqrt_fusion, f32[2304]{0:T(1024)S(1)} %broadcast_multiply_fusion.2, bf16[2,512,128]{2,1,0:T(8,128)(2,1)} %param.33, bf16[2,128,512]{2,1,0:T(8,128)(2,1)} %param.32), kind=kOutput, calls=%fused_computation.35 | convolution fusion | flops 616660992 | bytes 3236864 | tf_op jit(solution)/shard_map/dot_general | solution.py:108
  155.4 2.1 %copy.22 = bf16[2304,128]{1,0:T(8,128)(2,1)} copy(bf16[2304,128]{0,1:T(8,128)(2,1)} %fusion.27) | data formatting | bytes 1179648 | tf_op jit(solution)/shard_map/convert_element_type | solution.py:109
  (53 shorter events, 0.3 us)
Async XLA Ops:
  0.0 1.7 %copy-start = (bf16[9216,128]{1,0:T(8,128)(2,1)S(1)}, bf16[9216,128]{1,0:T(8,128)(2,1)}, u32[]{:S(2)}) copy-start(bf16[9216,128]{1,0:T(8,128)(2,1)} %param.17) | copy-start | bytes 7077892
  1.7 1.6 copy-start.13
  2.0 0.7 copy-start.18
  2.0 0.7 copy-start.19
  2.0 2.4 %copy-start.10 = (bf16[2,128,32]{1,2,0:T(8,128)(2,1)S(1)}, bf16[2,128,32]{1,2,0:T(8,128)(2,1)}, u32[]{:S(2)}) copy-start(bf16[2,128,32]{1,2,0:T(8,128)(2,1)} %param.21) | copy-start | bytes 49156
  2.0 12.1 %copy-start.16 = (f32[2,4]{1,0:T(2,128)S(1)}, f32[2,4]{1,0:T(2,128)}, u32[]{:S(2)}) copy-start(f32[2,4]{1,0:T(2,128)} %param.24) | copy-start | bytes 100
  14.1 1.9 %copy-start.7 = (bf16[2,128,128]{1,2,0:T(8,128)(2,1)}, bf16[2,128,128]{1,2,0:T(8,128)(2,1)S(1)}, u32[]{:S(2)}) copy-start(bf16[2,128,128]{1,2,0:T(8,128)(2,1)S(1)} %all_gather.9) | copy-start | bytes 196612
  16.0 2.3 %copy-start.11 = (bf16[2,128,32]{1,2,0:T(8,128)(2,1)S(1)}, bf16[2,128,32]{1,2,0:T(8,128)(2,1)}, u32[]{:S(2)}) copy-start(bf16[2,128,32]{1,2,0:T(8,128)(2,1)} %param.22) | copy-start | bytes 49156
  16.7 10.3 %copy-start.2 = (f32[2304,4,32]{0,2,1:T(8,128)S(1)}, f32[2304,4,32]{0,2,1:T(8,128)}, u32[]{:S(2)}) copy-start(f32[2304,4,32]{0,2,1:T(8,128)} %get-tuple-element.36) | copy-start | bytes 3538948
  26.5 1.1 copy-start.5
  27.0 40.9 %copy-start.23 = (bf16[2,32,32]{2,1,0:T(8,128)(2,1)S(1)}, bf16[2,32,32]{2,1,0:T(8,128)(2,1)}, u32[]{:S(2)}) copy-start(bf16[2,32,32]{2,1,0:T(8,128)(2,1)} %param.26) | copy-start | bytes 12292
  27.0 41.2 %copy-start.24 = (bf16[2,32,32]{2,1,0:T(8,128)(2,1)S(1)}, bf16[2,32,32]{2,1,0:T(8,128)(2,1)}, u32[]{:S(2)}) copy-start(bf16[2,32,32]{2,1,0:T(8,128)(2,1)} %param.25) | copy-start | bytes 12292
  27.0 41.7 %copy-start.25 = (bf16[2,32,32]{2,1,0:T(8,128)(2,1)S(1)}, bf16[2,32,32]{2,1,0:T(8,128)(2,1)}, u32[]{:S(2)}) copy-start(bf16[2,32,32]{2,1,0:T(8,128)(2,1)} %param.27) | copy-start | bytes 12292
  27.6 41.6 %copy-start.12 = (bf16[2,32,128]{2,1,0:T(8,128)(2,1)S(1)}, bf16[2,32,128]{2,1,0:T(8,128)(2,1)}, u32[]{:S(2)}) copy-start(bf16[2,32,128]{2,1,0:T(8,128)(2,1)} %param.28) | copy-start | bytes 49156
  27.6 51.2 %copy-start.17 = (f32[2,128]{1,0:T(2,128)S(1)}, f32[2,128]{1,0:T(2,128)}, u32[]{:S(2)}) copy-start(f32[2,128]{1,0:T(2,128)} %param.29) | copy-start | bytes 3076
  82.2 2.1 %copy-start.20 = (f32[2,128]{1,0:T(2,128)S(1)}, f32[2,128]{1,0:T(2,128)}, u32[]{:S(2)}) copy-start(f32[2,128]{1,0:T(2,128)} %param.31) | copy-start | bytes 3076
  82.2 2.1 %copy-start.21 = (f32[2,128]{1,0:T(2,128)S(1)}, f32[2,128]{1,0:T(2,128)}, u32[]{:S(2)}) copy-start(f32[2,128]{1,0:T(2,128)} %param.30) | copy-start | bytes 3076
  82.2 2.7 %copy-start.8 = (f32[2304]{0:T(1024)}, f32[2304]{0:T(1024)S(1)}, u32[]{:S(2)}) copy-start(f32[2304]{0:T(1024)S(1)} %broadcast_multiply_fusion.4) | copy-start | bytes 27652
  89.4 0.9 copy-start.14
  89.4 0.9 copy-start.15
  96.5 1.6 %copy-start.1 = (bf16[2304,128]{0,1:T(8,128)(2,1)S(1)}, bf16[2304,128]{0,1:T(8,128)(2,1)}, u32[]{:S(2)}) copy-start(bf16[2304,128]{0,1:T(8,128)(2,1)} %add_convert_fusion.1) | copy-start | bytes 1769476
  96.5 1.6 %copy-start.6 = (bf16[2,128,128]{1,2,0:T(8,128)(2,1)S(1)}, bf16[2,128,128]{1,2,0:T(8,128)(2,1)}, u32[]{:S(2)}) copy-start(bf16[2,128,128]{1,2,0:T(8,128)(2,1)} %copy-done.5) | copy-start | bytes 196612
  96.5 2.0 %copy-start.3 = (f32[2304,4,32]{0,2,1:T(8,128)S(1)}, f32[2304,4,32]{0,2,1:T(8,128)}, u32[]{:S(2)}) copy-start(f32[2304,4,32]{0,2,1:T(8,128)} %get-tuple-element.44) | copy-start | bytes 3538948
  96.5 2.0 %copy-start.9 = (f32[2304,4]{0,1:T(4,128)S(1)}, f32[2304,4]{0,1:T(4,128)}, u32[]{:S(2)}) copy-start(f32[2304,4]{0,1:T(4,128)} %get-tuple-element.43) | copy-start | bytes 110596
  148.6 2.8 %copy-start.4 = (f32[2304,128]{0,1:T(8,128)S(1)}, f32[2304,128]{0,1:T(8,128)}, u32[]{:S(2)}) copy-start(f32[2304,128]{0,1:T(8,128)} %get-tuple-element.48) | copy-start | bytes 3538948
  148.6 2.8 %copy-start.22 = (f32[128]{0:T(128)S(1)}, f32[128]{0:T(128)}, u32[]{:S(2)}) copy-start(f32[128]{0:T(128)} %get-tuple-element.23) | copy-start | bytes 1540
where the time goes:
time: 159 us; the launch traced here: 158 us
  blocking collectives  107 us (67%)
  matrix products  27.6 us (17%)
  other arithmetic  12.6 us (8%)
  local copies, waits for them, and re-layouts  8.79 us (6%)
    psum x2, blocking collectives, body(): numerator, total = lax.psum((numerator, total), ('pts', 'head'))  80.5 us
    all_gather x1, blocking collectives, body(): full_in = lax.all_gather(w_in, 'head', axis=2, tiled=True)  9.72 us
    all_gather x1, blocking collectives, body(): full_out = lax.all_gather(w_out, 'head', axis=1, tiled=True)  9 us
    dot_general x2, matrix products, body(): jnp.dot(upper, w_down[layer_index], preferred_element_type=jnp.float32)  8.51 us
    all_gather x1, blocking collectives, body(): full_fx = lax.all_gather(w_fx, 'head', axis=2, tiled=True)  8.21 us
    dot_general x2, matrix products, body(): projected = jnp.dot(half_weights, wide, preferred_element_type=jnp.float32)  6.22 us
    sub x2, matrix products, body(): weights = jax.nn.softmax(logits, axis=-1) * live[:, None, None]  5.29 us
    reduce_sum x2, other arithmetic, body(): total = jnp.sum(weights, axis=0)  3.22 us

commit v1 on v0

--- a/solution.py
+++ b/solution.py
@@ -55,7 +55,12 @@
     layers = w_in.shape[0]
     full_in = lax.all_gather(w_in, "head", axis=2, tiled=True)
     full_fx = lax.all_gather(w_fx, "head", axis=2, tiled=True)
-    full_out = lax.all_gather(w_out, "head", axis=1, tiled=True)
+    ring = [w_out]
+    for hop in range(3):
+        ring.append(lax.ppermute(ring[-1], "head", [(dev, (dev + 1) % 4) for dev in range(4)]))
+    full_out = jnp.roll(
+        jnp.concatenate(ring[::-1], axis=1), (lax.axis_index("head") + 1) * ring[0].shape[1], axis=1
+    )
     heads = full_in.shape[2] // DH
     live = (first_row + jnp.arange(rows, dtype=jnp.int32) < counts[0]).astype(jnp.float32)
     current = lax.dynamic_slice_in_dim(points, first_row, rows, 0)

time: 159 us -> 164 us (1.031)
  blocking collectives: 107 us -> 96.9 us
  starting transfers between devices: 0 us -> 6.71 us
  matrix products: 27.6 us -> 33.5 us
  waiting for transfers between devices: 0 us -> 3.96 us
    all_gather x1 -> x0, blocking collectives: 9 us -> none  [body(): full_out = lax.all_gather(w_out, 'head', axis=1, tiled=True)]
    ppermute x0 -> x3, starting transfers between devices: none -> 6.71 us  [body(): lax.ppermute(ring[-1], 'head', [(dev, (dev + 1) % 4) for dev in range(4)])]
    ppermute x0 -> x3, waiting for transfers between devices: none -> 3.96 us  [body(): lax.ppermute(ring[-1], 'head', [(dev, (dev + 1) % 4) for dev in range(4)])]
    dot_general x2, matrix products: 1.2 us -> 3.31 us  [body(): jnp.einsum('rs,rl->sl', half_weights, feats, preferred_element_type=jnp.f...]
  transfers between devices with their start and end apart: 0 -> 3, of which waited for: 0 -> 2; matrix products, arithmetic and copies ran while one was open for 0% -> 9% of each run, Pallas kernels for 0% -> 0%
where the time goes in v1:
time: 164 us; the launch traced here: 163 us
  blocking collectives  96.9 us (59%)
  matrix products  33.5 us (20%)
  other arithmetic  11.6 us (7%)
  local copies, waits for them, and re-layouts  8.91 us (5%)
  starting transfers between devices  6.71 us (4%)
  waiting for transfers between devices  3.96 us (2%)
    psum x2, blocking collectives, body(): numerator, total = lax.psum((numerator, total), ('pts', 'head'))  80.8 us
    dot_general x2, matrix products, body(): jnp.dot(upper, w_down[layer_index], preferred_element_type=jnp.float32)  8.53 us
    all_gather x1, blocking collectives, body(): full_in = lax.all_gather(w_in, 'head', axis=2, tiled=True)  8.24 us
    all_gather x1, blocking collectives, body(): full_fx = lax.all_gather(w_fx, 'head', axis=2, tiled=True)  7.81 us
    ppermute x3, starting transfers between devices, body(): lax.ppermute(ring[-1], 'head', [(dev, (dev + 1) % 4) for dev in range(4)])  6.71 us
    dot_general x2, matrix products, body(): projected = jnp.dot(half_weights, wide, preferred_element_type=jnp.float32)  6.26 us
    sub x2, matrix products, body(): weights = jax.nn.softmax(logits, axis=-1) * live[:, None, None]  5.24 us
    ppermute x3, waiting for transfers between devices, body(): lax.ppermute(ring[-1], 'head', [(dev, (dev + 1) % 4) for dev in range(4)])  3.96 us
  transfers between devices with their start and end apart: 3, of which 2 were waited for; matrix products, arithmetic and copies ran while one was open for 9% of the time, Pallas kernels for 0%

profile of v1, /device:TPU:0, one launch (start us, length us, event | category | flops | bytes accessed | tf_op | source)
XLA Modules:
  0.0 162.6 jit_solution(722386731942477610)
XLA Ops:
  0.0 3.0 %collective-permute-start = (bf16[2,32,128]{2,1,0:T(8,128)(2,1)}, bf16[2,32,128]{2,1,0:T(8,128)(2,1)}, u32[]{:S(2)}, u32[]{:S(2)}) collective-permute-start(bf16[2,32,128]{2,1,0:T(8,128)(2,1)} %param.28), channel_id=1, source_target_pairs={{0,1},{1,2},{2,3},{3,0},{4,5},{5,6},{6,7},{7,4},{8,9},{9,10},{10,1... | collective-permute-start | bytes 49160 | tf_op jit(solution)/shard_map/ppermute | solution.py:60
  3.0 0.6 fusion.102
  3.6 0.0 copy-start.13
  3.6 0.2 copy.26
  3.9 0.1 convert_reduce_fusion
  4.0 0.2 fusion.33
  4.2 0.1 copy-done.13
  4.3 0.1 copy.19
  4.4 0.1 copy.20
  4.5 0.1 copy-done.15
  4.5 0.2 broadcast_multiply_fusion
  4.7 0.1 mul.190
  4.8 8.2 %all_gather.6 = bf16[2,128,128]{1,2,0:T(8,128)(2,1)S(1)} all-gather(bf16[2,128,32]{1,2,0:T(8,128)(2,1)S(1)} %copy-done.11), channel_id=1, replica_groups=mesh['pts'=8,'head'=4] {'head'}, dimensions={2}, use_global_device_ids=true | all-gather | bytes 81920 | tf_op jit(solution)/shard_map/all_gather | solution.py:56
  13.1 0.6 slice_bitcast_fusion.33
  13.7 7.8 %all_gather.7 = bf16[2,128,128]{1,2,0:T(8,128)(2,1)S(1)} all-gather(bf16[2,128,32]{1,2,0:T(8,128)(2,1)S(1)} %copy-done.12), channel_id=1, replica_groups=mesh['pts'=8,'head'=4] {'head'}, dimensions={2}, use_global_device_ids=true | all-gather | bytes 81920 | tf_op jit(solution)/shard_map/all_gather | solution.py:57
  22.2 0.5 slice_bitcast_fusion.34
  22.7 1.2 convolution_convert_fusion.1
  24.0 1.8 %fusion.121 = (f32[2304,4]{0,1:T(4,128)S(1)}, f32[2304,4,32]{0,2,1:T(8,128)}) fusion(bf16[4,32,128]{2,1,0:T(8,128)(2,1)S(1)} %bitcast.210, f32[4]{0:T(128)S(1)} %get-tuple-element.28, bf16[2,128,128]{1,2,0:T(8,128)(2,1)S(1)} %all_gather.6, bf16[2304,128]{0,1:T(8,128)(2,1)S(1)} %copy.26, f32[128]{0:T(128)S(1)} %get-tuple-element.34, ...), kind=kOutput, calls=%fused_computation.184 | convolution fusion | flops 153944096 | bytes 1897984 | tf_op jit(solution)/shard_map/sub | solution.py:80
  25.8 1.6 fusion.57
  27.4 0.0 copy-done.2
  27.4 1.7 %fusion.39 = f32[4,32,4,32]{3,1,2,0:T(8,128)S(1)} fusion(bf16[4,32,2304,1]{2,1,0,3:T(8,128)(2,1)} %bitcast.213, f32[2304]{0:T(1024)S(1)} %fusion.83, f32[2304,4,32]{0,2,1:T(8,128)S(1)} %copy-done.2, f32[2304,4]{0,1:T(4,128)S(1)} %get-tuple-element.35), kind=kOutput, calls=%fused_computation.67 | convolution fusion | flops 76382208 | bytes 1881088 | tf_op jit(solution)/shard_map/rs,rl->sl/dot_general | solution.py:83
  29.2 40.2 %all-reduce.1 = (f32[4,32,32]{2,1,0:T(8,128)S(1)}, f32[4,32]{1,0:T(4,128)S(1)}) all-reduce(f32[4,32,32]{2,1,0:T(8,128)S(1)} %pad_maximum_fusion, f32[4,32]{1,0:T(4,128)S(1)} %fusion.57), channel_id=1, replica_groups=mesh['pts'=8,'head'=4] {'pts','head'}, use_global_device_ids=true, to_apply=%region_4.5 | all-reduce | flops 4224 | bytes 33792 | tf_op jit(solution)/shard_map/psum | solution.py:86
  69.4 0.9 fusion.92
  70.3 0.9 fusion.94
  71.3 0.9 fusion.90
  72.2 0.2 fusion.124
  72.5 0.3 convolution_convert_fusion.7
  72.8 2.3 %collective-permute-start.1 = (bf16[2,32,128]{2,1,0:T(8,128)(2,1)}, bf16[2,32,128]{2,1,0:T(8,128)(2,1)S(1)}, u32[]{:S(2)}, u32[]{:S(2)}) collective-permute-start(bf16[2,32,128]{2,1,0:T(8,128)(2,1)} %collective-permute-done), channel_id=1, source_target_pairs={{0,1},{1,2},{2,3},{3,0},{4,5},{5,6},{6,7},{7,4},{8,9},{9,10},{10,1... | collective-permute-start | bytes 49160 | tf_op jit(solution)/shard_map/ppermute | solution.py:60
  75.1 0.6 slice_bitcast_fusion.30
  75.7 2.0 %collective-permute-done.1 = bf16[2,32,128]{2,1,0:T(8,128)(2,1)S(1)} collective-permute-done((bf16[2,32,128]{2,1,0:T(8,128)(2,1)}, bf16[2,32,128]{2,1,0:T(8,128)(2,1)S(1)}, u32[]{:S(2)}, u32[]{:S(2)}) %collective-permute-start.1) | collective-permute-done | bytes 16416 | tf_op jit(solution)/shard_map/ppermute | solution.py:60
  77.7 1.4 collective-permute-start.2
  79.1 0.5 slice_bitcast_fusion.32
  79.6 0.7 mul.214
  80.4 2.0 %collective-permute-done.2 = bf16[2,32,128]{2,1,0:T(8,128)(2,1)S(1)} collective-permute-done((bf16[2,32,128]{2,1,0:T(8,128)(2,1)S(1)}, bf16[2,32,128]{2,1,0:T(8,128)(2,1)S(1)}, u32[]{:S(2)}, u32[]{:S(2)}) %collective-permute-start.2) | collective-permute-done | bytes 16416 | tf_op jit(solution)/shard_map/ppermute | solution.py:60
  82.4 0.7 constant_dynamic-update-slice_fusion.5
  83.1 0.7 constant_dynamic-update-slice_fusion.1
  83.9 0.6 constant_dynamic-slice_fusion.1
  84.5 2.8 %fusion.125 = (f32[2304]{0:T(1024)S(1)}, f32[2304,128]{0,1:T(8,128)}) fusion(f32[128]{0:T(128)S(1)} %get-tuple-element.26, bf16[4,32,32]{2,1,0:T(8,128)(2,1)S(1)} %convolution_convert_fusion.7, bf16[4,32,128]{2,1,0:T(8,128)(2,1)S(1)} %bitcast.212, f32[2304]{0:T(1024)S(1)} %fusion.83, f32[2304,4,32]{0,2,1:T(8,128)} %get-tuple-element.36, ...), kind=kOutput, calls=%fused_computation.186 | convolution fusion | flops 78624512 | bytes 3045888 | tf_op jit(solution)/shard_map/dot_general | solution.py:104
  87.3 1.4 multiply_reduce_fusion.2
  88.7 0.6 add_rsqrt_fusion.2
  89.3 4.6 %fusion.126 = (f32[2304]{0:T(1024)}, f32[2304,128]{0,1:T(8,128)S(1)}) fusion(f32[2304,128]{0,1:T(8,128)} %get-tuple-element.40, bf16[2,512,128]{2,1,0:T(8,128)(2,1)} %param.33, f32[128]{0:T(128)} %get-tuple-element.24, f32[128]{0:T(128)} %get-tuple-element.51, f32[2304]{0:T(1024)} %add_rsqrt_fusion.2, f32[2304]{0:T(1024)} %copy-done.9, ...), kind=kOutput, calls=%fused_computation.187 | convolution fusion | flops 617248512 | bytes 3835904 | tf_op jit(solution)/shard_map/dot_general | solution.py:113
  93.9 0.7 broadcast_multiply_fusion.3
  94.6 0.1 multiply_reduce_fusion.1
  94.8 0.4 add_convert_fusion.1
  95.2 0.8 copy-done.1
  96.0 1.1 convolution_convert_fusion
  97.1 3.4 %fusion.129 = (f32[2304,4]{0,1:T(4,128)}, f32[2304,4,32]{0,2,1:T(8,128)}) fusion(bf16[4,32,128]{2,1,0:T(8,128)(2,1)} %bitcast.209, bf16[2304,128]{0,1:T(8,128)(2,1)} %copy-done.1, f32[4]{0:T(128)S(1)} %copy-done.22, bf16[2,128,128]{1,2,0:T(8,128)(2,1)} %copy-done.7), kind=kOutput, calls=%fused_computation.188 | convolution fusion | flops 152174624 | bytes 1871888 | tf_op jit(solution)/shard_map/sub | solution.py:80
  100.5 1.6 fusion.59
  102.1 0.0 copy-done.3
  102.2 1.7 %fusion.37 = f32[4,32,4,32]{3,1,2,0:T(8,128)S(1)} fusion(bf16[4,32,2304,1]{2,1,0,3:T(8,128)(2,1)} %bitcast.208, f32[2304]{0:T(1024)S(1)} %fusion.83, f32[2304,4,32]{0,2,1:T(8,128)S(1)} %copy-done.3, f32[2304,4]{0,1:T(4,128)S(1)} %copy-done.10), kind=kOutput, calls=%fused_computation.65 | convolution fusion | flops 76382208 | bytes 1881088 | tf_op jit(solution)/shard_map/rs,rl->sl/dot_general | solution.py:83
  103.9 0.6 pad_maximum_fusion.1
  104.5 40.6 %all-reduce = (f32[4,32,32]{2,1,0:T(8,128)}, f32[4,32]{1,0:T(4,128)}) all-reduce(f32[4,32,32]{2,1,0:T(8,128)} %pad_maximum_fusion.1, f32[4,32]{1,0:T(4,128)S(1)} %fusion.59), channel_id=1, replica_groups=mesh['pts'=8,'head'=4] {'pts','head'}, use_global_device_ids=true, to_apply=%region_15.16 | all-reduce | flops 4224 | bytes 33792 | tf_op jit(solution)/shard_map/psum | solution.py:86
  145.1 0.7 broadcast_maximum_fusion
  145.8 1.1 fusion.86
  146.9 1.1 fusion.88
  147.9 1.1 fusion.84
  149.0 0.2 fusion.130
  149.3 0.9 convolution_convert_fusion.5
  150.2 3.4 %fusion.131 = (f32[2304]{0:T(1024)}, f32[2304,128]{0,1:T(8,128)}) fusion(f32[128]{0:T(128)} %get-tuple-element.25, f32[2304,128]{0,1:T(8,128)S(1)} %get-tuple-element.42, bf16[4,32,32]{2,1,0:T(8,128)(2,1)} %convolution_convert_fusion.5, bf16[4,32,128]{2,1,0:T(8,128)(2,1)} %bitcast.211, f32[2304]{0:T(1024)S(1)} %fusion.83, ...), kind=kOutput, calls=%fused_computation.190 | convolution fusion | flops 78329600 | bytes 3635712 | tf_op jit(solution)/shard_map/dot_general | solution.py:104
  153.7 0.8 broadcast_multiply_fusion.2
  154.5 1.4 multiply_reduce_fusion
  155.9 0.6 add_rsqrt_fusion
  156.5 4.0 %fusion.27 = bf16[2304,128]{0,1:T(8,128)(2,1)} fusion(f32[2304,128]{0,1:T(8,128)S(1)} %copy-done.4, f32[128]{0:T(128)S(1)} %copy-done.23, f32[128]{0:T(128)} %get-tuple-element.52, f32[2304]{0:T(1024)} %add_rsqrt_fusion, f32[2304]{0:T(1024)S(1)} %broadcast_multiply_fusion.2, bf16[2,512,128]{2,1,0:T(8,128)(2,1)} %param.33, bf16[2,128,512]{2,1,0:T(8,128)(2,1)} %param.32), kind=kOutput, calls=%fused_computation.35 | convolution fusion | flops 616660992 | bytes 3236864 | tf_op jit(solution)/shard_map/dot_general | solution.py:113
  160.5 2.1 %copy.22 = bf16[2304,128]{1,0:T(8,128)(2,1)} copy(bf16[2304,128]{0,1:T(8,128)(2,1)} %fusion.27) | data formatting | bytes 1179648 | tf_op jit(solution)/shard_map/convert_element_type | solution.py:114
  (62 shorter events, 0.3 us)
Async XLA Ops:
  0.0 3.5 %copy-start = (bf16[9216,128]{1,0:T(8,128)(2,1)S(1)}, bf16[9216,128]{1,0:T(8,128)(2,1)}, u32[]{:S(2)}) copy-start(bf16[9216,128]{1,0:T(8,128)(2,1)} %param.17) | copy-start | bytes 7077892
  0.0 72.8 %collective-permute-start = (bf16[2,32,128]{2,1,0:T(8,128)(2,1)}, bf16[2,32,128]{2,1,0:T(8,128)(2,1)}, u32[]{:S(2)}, u32[]{:S(2)}) collective-permute-start(bf16[2,32,128]{2,1,0:T(8,128)(2,1)} %param.28), channel_id=1, source_target_pairs={{0,1},{1,2},{2,3},{3,0},{4,5},{5,6},{6,7},{7,4},{8,9},{9,10},{10,1... | collective-permute-start | bytes 49160 | tf_op jit(solution)/shard_map/ppermute | solution.py:60
  3.6 0.7 copy-start.13
  3.8 0.7 copy-start.15
  3.9 1.0 copy-start.11
  3.9 9.2 %copy-start.16 = (f32[2,4]{1,0:T(2,128)S(1)}, f32[2,4]{1,0:T(2,128)}, u32[]{:S(2)}) copy-start(f32[2,4]{1,0:T(2,128)} %param.24) | copy-start | bytes 100
  3.9 9.8 %copy-start.12 = (bf16[2,128,32]{1,2,0:T(8,128)(2,1)S(1)}, bf16[2,128,32]{1,2,0:T(8,128)(2,1)}, u32[]{:S(2)}) copy-start(bf16[2,128,32]{1,2,0:T(8,128)(2,1)} %param.22) | copy-start | bytes 49156
  3.9 18.3 %copy-start.18 = (f32[2,128]{1,0:T(2,128)S(1)}, f32[2,128]{1,0:T(2,128)}, u32[]{:S(2)}) copy-start(f32[2,128]{1,0:T(2,128)} %param.20) | copy-start | bytes 3076
  3.9 18.3 %copy-start.19 = (f32[2,128]{1,0:T(2,128)S(1)}, f32[2,128]{1,0:T(2,128)}, u32[]{:S(2)}) copy-start(f32[2,128]{1,0:T(2,128)} %param.19) | copy-start | bytes 3076
  13.1 12.7 %copy-start.7 = (bf16[2,128,128]{1,2,0:T(8,128)(2,1)}, bf16[2,128,128]{1,2,0:T(8,128)(2,1)S(1)}, u32[]{:S(2)}) copy-start(bf16[2,128,128]{1,2,0:T(8,128)(2,1)S(1)} %all_gather.6) | copy-start | bytes 196612
  21.5 1.2 copy-start.5
  25.8 1.6 %copy-start.2 = (f32[2304,4,32]{0,2,1:T(8,128)S(1)}, f32[2304,4,32]{0,2,1:T(8,128)}, u32[]{:S(2)}) copy-start(f32[2304,4,32]{0,2,1:T(8,128)} %get-tuple-element.36) | copy-start | bytes 3538948
  29.1 50.1 %copy-start.17 = (f32[2,128]{1,0:T(2,128)S(1)}, f32[2,128]{1,0:T(2,128)}, u32[]{:S(2)}) copy-start(f32[2,128]{1,0:T(2,128)} %param.29) | copy-start | bytes 3076
  29.1 54.0 %copy-start.8 = (bf16[2,32,128]{2,1,0:T(8,128)(2,1)S(1)}, bf16[2,32,128]{2,1,0:T(8,128)(2,1)}, u32[]{:S(2)}) copy-start(bf16[2,32,128]{2,1,0:T(8,128)(2,1)} %param.28) | copy-start | bytes 49156
  29.1 46.0 %copy-start.20 = (f32[2,128]{1,0:T(2,128)S(1)}, f32[2,128]{1,0:T(2,128)}, u32[]{:S(2)}) copy-start(f32[2,128]{1,0:T(2,128)} %param.31) | copy-start | bytes 3076
  29.1 46.0 %copy-start.21 = (f32[2,128]{1,0:T(2,128)S(1)}, f32[2,128]{1,0:T(2,128)}, u32[]{:S(2)}) copy-start(f32[2,128]{1,0:T(2,128)} %param.30) | copy-start | bytes 3076
  72.8 4.9 %collective-permute-start.1 = (bf16[2,32,128]{2,1,0:T(8,128)(2,1)}, bf16[2,32,128]{2,1,0:T(8,128)(2,1)S(1)}, u32[]{:S(2)}, u32[]{:S(2)}) collective-permute-start(bf16[2,32,128]{2,1,0:T(8,128)(2,1)} %collective-permute-done), channel_id=1, source_target_pairs={{0,1},{1,2},{2,3},{3,0},{4,5},{5,6},{6,7},{7,4},{8,9},{9,10},{10,1... | collective-permute-start | bytes 49160 | tf_op jit(solution)/shard_map/ppermute | solution.py:60
  77.7 4.6 %collective-permute-start.2 = (bf16[2,32,128]{2,1,0:T(8,128)(2,1)S(1)}, bf16[2,32,128]{2,1,0:T(8,128)(2,1)S(1)}, u32[]{:S(2)}, u32[]{:S(2)}) collective-permute-start(bf16[2,32,128]{2,1,0:T(8,128)(2,1)S(1)} %collective-permute-done.1), channel_id=1, source_target_pairs={{0,1},{1,2},{2,3},{3,0},{4,5},{5,6},{6,7},{7,4},{8,9},{9,10},{10,1... | collective-permute-start | bytes 49160 | tf_op jit(solution)/shard_map/ppermute | solution.py:60
  87.3 2.0 %copy-start.9 = (f32[2304]{0:T(1024)}, f32[2304]{0:T(1024)S(1)}, u32[]{:S(2)}) copy-start(f32[2304]{0:T(1024)S(1)} %broadcast_multiply_fusion.4) | copy-start | bytes 27652
  93.9 0.9 copy-start.14
  94.7 1.3 copy-start.6
  95.1 0.8 copy-start.1
  96.0 1.1 copy-start.22
  100.5 1.6 %copy-start.3 = (f32[2304,4,32]{0,2,1:T(8,128)S(1)}, f32[2304,4,32]{0,2,1:T(8,128)}, u32[]{:S(2)}) copy-start(f32[2304,4,32]{0,2,1:T(8,128)} %get-tuple-element.44) | copy-start | bytes 3538948
  100.5 1.6 %copy-start.10 = (f32[2304,4]{0,1:T(4,128)S(1)}, f32[2304,4]{0,1:T(4,128)}, u32[]{:S(2)}) copy-start(f32[2304,4]{0,1:T(4,128)} %get-tuple-element.43) | copy-start | bytes 110596
  153.7 2.8 %copy-start.4 = (f32[2304,128]{0,1:T(8,128)S(1)}, f32[2304,128]{0,1:T(8,128)}, u32[]{:S(2)}) copy-start(f32[2304,128]{0,1:T(8,128)} %get-tuple-element.48) | copy-start | bytes 3538948
  153.7 2.8 %copy-start.23 = (f32[128]{0:T(128)S(1)}, f32[128]{0:T(128)}, u32[]{:S(2)}) copy-start(f32[128]{0:T(128)} %get-tuple-element.23) | copy-start | bytes 1540
